TPU v7x, 16 devices: a 4x2x1 block of a 4x4x4 slice. The times are simulated.
16 devices in a mesh: dp: 2 (over y, z), tp: 8 (over x, core).
Axes of the slice: x: 4, y: 2, z: 1, core: 2. Of those that a mesh axis runs over, the one named last changes fastest.
The devices are a block of a 4x4x4 slice.
Arguments:
- x: bfloat16 [128, 8192], P('dp'), parts along dimension 0
- k_cache: bfloat16 [128, 4096, 8, 128], P('dp', None, 'tp'), parts along dimension 0
- v_cache: bfloat16 [128, 4096, 8, 128], P('dp', None, 'tp'), parts along dimension 0
- gain_a: bfloat16 [8192], replicated
- wq: bfloat16 [8192, 8192], P(None, 'tp')
- wo: bfloat16 [8192, 8192], P('tp')
- gain_m: bfloat16 [8192], replicated
- w_gate: bfloat16 [8192, 49152], P(None, 'tp')
- w_up: bfloat16 [8192, 49152], P(None, 'tp')
- w_down: bfloat16 [49152, 8192], P('tp')
Outputs:
- output: bfloat16 [128, 8192], P('dp'), parts along dimension 0
There are 2 independent parts. A program takes and returns all parts, laid end to end along the dimension named above; an argument that names none is the same for every part.
All inputs are finite; a program needn't handle non-finite values.
Results may differ from a plain program's by a relative error of at most 0.017.
Values are sent between devices in bfloat16 or wider.
A program may use at most 1.5 GiB of HBM per device.

v0:
```python
import jax
import jax.numpy as jnp
from jax import lax
from jax.sharding import PartitionSpec as P

HEAD = 128
THETA = 10000


def normed(x, gain):
    wide = x.astype(jnp.float32)
    scale = lax.rsqrt(jnp.mean(wide * wide, -1, keepdims=True) + 1e-6)
    return (wide * scale * gain.astype(jnp.float32)).astype(jnp.bfloat16)


def turned(t, place, theta):
    half = t.shape[-1] // 2
    angle = place.astype(jnp.float32)[:, None] * theta ** (-jnp.arange(half, dtype=jnp.float32) / half)
    cos, sin = jnp.cos(angle)[:, None], jnp.sin(angle)[:, None]
    a, b = t[..., :half].astype(jnp.float32), t[..., half:].astype(jnp.float32)
    return jnp.concatenate([a * cos - b * sin, b * cos + a * sin], -1).astype(jnp.bfloat16)


def matmul(a, w):
    return jnp.dot(a, w, preferred_element_type=jnp.float32).astype(jnp.bfloat16)


def einsum(form, a, b):
    return jnp.einsum(form, a.astype(jnp.float32), b.astype(jnp.float32))


def seen_by(a, wq, k_cache, v_cache, head, theta):
    batch, cache, kv_heads = k_cache.shape[:3]
    place = jnp.full((batch,), cache - 1)
    q = turned(matmul(a, wq).reshape(batch, -1, head), place, theta).reshape(batch, kv_heads, -1, head)
    scores = einsum("bgsd,bugd->bgsu", q, k_cache) * head**-0.5
    weights = jax.nn.softmax(scores, -1).astype(jnp.bfloat16)
    return einsum("bgsu,bugd->bgsd", weights, v_cache).astype(jnp.bfloat16).reshape(batch, -1)


def hidden_of(b, w_gate, w_up):
    gate = jnp.dot(b, w_gate, preferred_element_type=jnp.float32)
    up = jnp.dot(b, w_up, preferred_element_type=jnp.float32)
    return (jax.nn.silu(gate) * up).astype(jnp.bfloat16)


def solution(mesh):
    def added(t, term):
        return (t.astype(jnp.float32) + lax.psum(term.astype(jnp.bfloat16), "tp").astype(jnp.float32)).astype(jnp.bfloat16)

    def step(x, k_cache, v_cache, gain_a, wq, wo, gain_m, w_gate, w_up, w_down):
        seen = seen_by(normed(x, gain_a), wq, k_cache, v_cache, HEAD, THETA)
        h = added(x, jnp.dot(seen, wo, preferred_element_type=jnp.float32))
        return added(h, jnp.dot(hidden_of(normed(h, gain_m), w_gate, w_up), w_down, preferred_element_type=jnp.float32))

    states, cache, columns, rows_of = P("dp", None), P("dp", None, "tp", None), P(None, "tp"), P("tp", None)
    return jax.shard_map(
        step,
        mesh=mesh,
        in_specs=(states, cache, cache, P(None), columns, rows_of, P(None), columns, columns, rows_of),
        out_specs=states,
        check_vma=False,
    )
```

profile of v0, /device:TPU:113, one launch (start us, length us, event | category | flops | bytes accessed | tf_op | source)
XLA Modules:
  0.0 307.5 jit_solution(792244310425986906)
XLA Ops:
  6.5 0.0 all-reduce.3.cloned.1.call-start
  6.6 0.7 convert_element_type.66
  7.3 1.5 fusion.9
  8.9 9.2 %fusion.25 = bf16[8,8,8,128]{3,1,2,0:T(8,128)(2,1)S(1)} fusion(bf16[8192,1024]{1,0:T(8,128)(2,1)} %param.14, bf16[64,8192]{1,0:T(8,128)(2,1)} %param.10, f32[8192]{0:T(1024)S(1)} %convert_element_type.66, f32[64]{0:T(128)S(1)} %add_rsqrt_fusion.1), kind=kOutput, calls=%fused_computation.36 | convolution fusion | flops 1075904512 | bytes 17989888 | tf_op jit(solution)/shard_map/dot_general | solution.py:25
  18.1 0.1 fusion.35
  18.3 29.1 %fusion.49 = (f32[64,8]{1,0:T(8,128)S(1)}, f32[64,8,4096]{2,1,0:T(8,128)}) fusion(bf16[64,4096,1,128]{3,1,2,0:T(8,128)(2,1)} %param.11, bf16[64,8,64]{2,1,0:T(8,128)(2,1)S(1)} %get-tuple-element.8, bf16[64,8,64]{2,1,0:T(8,128)(2,1)S(1)} %get-tuple-element.7), kind=kOutput, calls=%fused_computation.62 | convolution fusion | flops 543428608 | bytes 75630592 | tf_op jit(solution)/shard_map/sub | solution.py:37
  47.4 25.1 %fusion.22 = bf16[64,8,128]{2,1,0:T(8,128)(2,1)S(1)} fusion(bf16[64,4096,1,128]{3,1,2,0:T(8,128)(2,1)} %param.12, f32[64,8,4096]{2,1,0:T(8,128)} %get-tuple-element.10, f32[64,8]{1,0:T(8,128)S(1)} %get-tuple-element.9), kind=kOutput, calls=%fused_computation.34 | convolution fusion | flops 541130752 | bytes 75630592 | tf_op jit(solution)/shard_map/bgsu,bugd->bgsd/dot_general | solution.py:29
  72.6 0.0 copy-start.1
  72.6 0.0 copy-start
  72.6 9.9 %convolution_convert_fusion.1 = bf16[64,8192]{1,0:T(8,128)(2,1)} fusion(bf16[1024,8192]{1,0:T(8,128)(2,1)} %param.15, bf16[8,8,8,128]{3,2,1,0:T(8,128)(2,1)S(1)} %bitcast.30), kind=kOutput, calls=%fused_computation.6 | convolution fusion | flops 1074266112 | bytes 17956864 | tf_op jit(solution)/shard_map/dot_general | solution.py:53
  82.4 0.1 all-reduce.3.cloned.1.call-update
  82.5 0.2 all-reduce.5.cloned.1.call-start
  82.7 0.0 copy-done.1
  82.8 55.0 %all-reduce.3.cloned.1.call-done = bf16[64,8192]{1,0:T(8,128)(2,1)} async-done(((bf16[64,8192]{1,0:T(8,128)(2,1)}), bf16[64,8192]{1,0:T(8,128)(2,1)}) %all-reduce.3.cloned.1.call-update) | async-done | bytes 1048592 | tf_op jit(solution)/shard_map/psum | solution.py:49
  137.8 0.0 copy-done
  137.8 1.7 fusion.13
  139.5 34.5 %fusion.32 = f32[64,6144]{1,0:T(8,128)S(1)} fusion(bf16[8192,6144]{1,0:T(8,128)(2,1)} %param.17, bf16[64,8192]{1,0:T(8,128)(2,1)S(1)} %get-tuple-element.6, f32[8192]{0:T(1024)S(1)} %convert_element_type.77, f32[64]{0:T(128)S(1)} %add_rsqrt_fusion), kind=kOutput, calls=%fused_computation.44 | convolution fusion | flops 6444548096 | bytes 103317760 | tf_op jit(solution)/shard_map/dot_general | solution.py:42
  174.0 34.9 %fusion.6.clone.4 = bf16[64,6144]{1,0:T(8,128)(2,1)S(1)} fusion(bf16[8192,6144]{1,0:T(8,128)(2,1)} %param.18, f32[64,6144]{1,0:T(8,128)S(1)} %fusion.32, bf16[64,8192]{1,0:T(8,128)(2,1)S(1)} %get-tuple-element.6, f32[8192]{0:T(1024)S(1)} %convert_element_type.77, f32[64]{0:T(128)S(1)} %add_rsqrt_fusion), kind=kOutput, calls=%fused_computation.12.clone.clone.clone.1 | convolution fusion | flops 6446907392 | bytes 104104192 | tf_op jit(solution)/shard_map/dot_general | solution.py:43
  209.0 35.5 %convolution_convert_fusion = bf16[64,8192]{1,0:T(8,128)(2,1)} fusion(bf16[6144,8192]{1,0:T(8,128)(2,1)} %param.19, bf16[64,6144]{1,0:T(8,128)(2,1)S(1)} %fusion.6.clone.4), kind=kOutput, calls=%fused_computation.5 | convolution fusion | flops 6442975232 | bytes 102498304 | tf_op jit(solution)/shard_map/dot_general | solution.py:54
  244.4 0.1 all-reduce.5.cloned.1.call-update
  244.5 53.7 %all-reduce.5.cloned.1.call-done = bf16[64,8192]{1,0:T(8,128)(2,1)} async-done(((bf16[64,8192]{1,0:T(8,128)(2,1)}), bf16[64,8192]{1,0:T(8,128)(2,1)}) %all-reduce.5.cloned.1.call-update) | async-done | bytes 1048592 | tf_op jit(solution)/shard_map/psum | solution.py:49
  298.2 2.4 fusion.16
  (5 shorter events, 0.1 us)
Async XLA Ops:
  6.5 131.2 %all-reduce.3.cloned.1.call-start = ((), (), s32[]{:S(2)}) async-start(), calls=%async_computation | async-start | bytes 2097152 | tf_op jit(solution)/shard_map/psum | solution.py:49
  72.6 10.2 %copy-start.1 = (bf16[8192]{0:T(1024)(128)(2,1)S(1)}, bf16[8192]{0:T(1024)(128)(2,1)}, u32[]{:S(2)}) copy-start(bf16[8192]{0:T(1024)(128)(2,1)} %param.16) | copy-start | bytes 49156
  72.6 65.2 %copy-start = (bf16[64,8192]{1,0:T(8,128)(2,1)S(1)}, bf16[64,8192]{1,0:T(8,128)(2,1)}, u32[]{:S(2)}) copy-start(bf16[64,8192]{1,0:T(8,128)(2,1)} %param.10) | copy-start | bytes 3145732
  82.5 215.7 %all-reduce.5.cloned.1.call-start = ((), (), s32[]{:S(2)}) async-start(), calls=%async_computation.1 | async-start | bytes 2097152 | tf_op jit(solution)/shard_map/psum | solution.py:49
Sparse Core Ops, SparseCore 0:
  82.6 55.1 all-reduce.2
  244.6 53.5 all-reduce.4
where the time goes:
time: 310 us; the launch traced here: 307 us
  matrix products  178 us (57%)
  waiting for transfers between devices  109 us (35%)
  between operations  13.5 us (4%)
  other arithmetic  6.58 us (2%)
    psum x2, waiting for transfers between devices, added(): lax.psum(term.astype(jnp.bfloat16), 'tp').astype(jnp.float32)  109 us
    dot_general x1, matrix products, step(): jnp.dot(hidden_of(normed(h, gain_m), w_gate, w_up), w_down, preferred_ele...  35.5 us
    dot_general x1, matrix products, hidden_of(): up = jnp.dot(b, w_up, preferred_element_type=jnp.float32)  34.9 us
    dot_general x1, matrix products, hidden_of(): gate = jnp.dot(b, w_gate, preferred_element_type=jnp.float32)  34.5 us
    sub x1, matrix products, seen_by(): weights = jax.nn.softmax(scores, -1).astype(jnp.bfloat16)  29.1 us
    dot_general x1, matrix products, einsum(): return jnp.einsum(form, a.astype(jnp.float32), b.astype(jnp.float32))  25.1 us
    dot_general x1, matrix products, step(): h = added(x, jnp.dot(seen, wo, preferred_element_type=jnp.float32))  9.85 us
    dot_general x1, matrix products, matmul(): jnp.dot(a, w, preferred_element_type=jnp.float32).astype(jnp.bfloat16)  9.22 us
  transfers between devices with their start and end apart: 2, of which 2 were waited for; matrix products, arithmetic and copies ran while one was open for 0% of the time, Pallas kernels for 0%

commit v1 on v0

v1 whole, which is shorter than its diff:
```python
import functools

import jax
import jax.numpy as jnp
import numpy as np
from jax import lax
from jax.experimental import pallas as pl
from jax.experimental.pallas import tpu as pltpu
from jax.sharding import PartitionSpec as P

HEAD = 128
THETA = 10000
LANES = 128
WIDTH = 256
SLOTS = 12
CORES = 2
F32, BF16 = jnp.float32, jnp.bfloat16
MESH = pl.DeviceIdType.MESH


def layer(n, dims, x_hbm, k_hbm, v_hbm, ga_ref, gm_ref, rot_ref, wq_hbm, wo_hbm, wg_hbm, wu_hbm, wd_hbm, y_ref,
          ring, xbuf, normed, hbuf, gain, q, seen, seen_bf, hidden, pbuf, sbuf, dbuf, tbuf, rbuf,
          ring_sem, x_sem, s_a, r_a, s_b, r_b, s_c, r_c, s_d, r_d):
    rows, d, cache, qcols, ff = dims
    heads = qcols // HEAD
    half_cache = cache // 2
    group = d // half_cache
    chips = n // CORES
    chunk = CORES * chips * LANES
    chunks = d // chunk
    core_cols = chips * LANES
    wo_cols = d // qcols * WIDTH
    per_item = wo_cols // chunk

    n_q, n_kv, n_wo, n_gu, n_wd = qcols // WIDTH, 2 * rows // group, d // wo_cols, 2 * ff // WIDTH, d // WIDTH
    kv0 = n_q
    wo0 = kv0 + n_kv
    gu0 = wo0 + n_wo
    wd0 = gu0 + n_gu
    end = wd0 + n_wd

    me = lax.axis_index("tp")
    chip, core = me // CORES, me % CORES
    partner = chip * CORES + (1 - core)

    def peer(distance):
        return lax.rem(chip + distance, chips) * CORES + core

    def columns(start, size):
        return pl.ds(pl.multiple_of(start, size), size)

    def slot(i):
        return i % SLOTS if isinstance(i, int) else lax.rem(i, SLOTS)

    def issue(i, phases):
        s = slot(i)
        sem = ring_sem.at[s]

        def cols_of(w, block, height):
            pltpu.make_async_copy(w.at[:, columns(block * WIDTH, WIDTH)], ring.at[s, pl.ds(0, height)], sem).start()

        def caches(src, g):
            for t in range(group):
                for h in range(2):
                    pltpu.make_async_copy(
                        src.at[g * group + t, pl.ds(h * half_cache, half_cache)],
                        ring.at[s, pl.ds(t * half_cache, half_cache), pl.ds(h * HEAD, HEAD)],
                        sem,
                    ).start()

        def wo_blocks(w):
            for m in range(wo_cols // WIDTH):
                pltpu.make_async_copy(
                    wo_hbm.at[:, columns(w * wo_cols + m * WIDTH, WIDTH)], ring.at[s, pl.ds(m * qcols, qcols)], sem
                ).start()

        def when(low, high, body):
            if isinstance(i, int):
                if low <= i < high:
                    body()
            else:
                pl.when((i >= low) & (i < high))(body)

        def either(first, second, j):
            if isinstance(j, int):
                (second if j % 2 else first)(j // 2)
            else:
                pl.when(j % 2 == 0)(lambda: first(j // 2))
                pl.when(j % 2 == 1)(lambda: second(j // 2))

        if "q" in phases:
            when(0, kv0, lambda: cols_of(wq_hbm, i, d))
        if "kv" in phases:
            when(kv0, wo0, lambda: either(lambda g: caches(k_hbm, g), lambda g: caches(v_hbm, g), i - kv0))
        if "wo" in phases:
            when(wo0, gu0, lambda: wo_blocks(i - wo0))
        if "gu" in phases:
            when(gu0, wd0, lambda: either(lambda j: cols_of(wg_hbm, j, d), lambda j: cols_of(wu_hbm, j, d), i - gu0))
        if "wd" in phases:
            when(wd0, end, lambda: cols_of(wd_hbm, i - wd0, ff))

    def arrived(i, height=d):
        s = slot(i)
        src = wd_hbm if height == ff else wg_hbm
        pltpu.make_async_copy(src.at[:, pl.ds(0, WIDTH)], ring.at[s, pl.ds(0, height)], ring_sem.at[s]).wait()
        return s

    def product(a_ref, s, depth, start=0, step=2048):
        total = None
        for k in range(0, depth, step):
            size = min(step, depth - k)
            part = jnp.dot(a_ref[:, k : k + size], ring[s, start + k : start + k + size], preferred_element_type=F32)
            total = part if total is None else total + part
        return total

    barrier = pltpu.get_barrier_semaphore()
    for device in [partner] + [peer(dist) for dist in range(1, chips)]:
        pl.semaphore_signal(barrier, inc=1, device_id={"tp": device}, device_id_type=MESH)
    x_copy = pltpu.make_async_copy(x_hbm, xbuf, x_sem)
    x_copy.start()
    for i in range(SLOTS):
        issue(i, ("q", "kv"))

    def norm(src_ref, gain_ref):
        gain[...] = gain_ref[...].astype(F32)
        block = 2 * LANES

        def square(r, acc):
            v = src_ref[:, columns(r * block, block)].astype(F32)
            v = v * v
            return acc + (v[:, :LANES] + v[:, LANES:])

        acc = lax.fori_loop(0, d // block, square, jnp.zeros((rows, LANES), F32), unroll=4)
        scale = lax.rsqrt(jnp.sum(acc, -1, keepdims=True) * (1.0 / d) + 1e-6)
        scale = jnp.broadcast_to(scale, (rows, LANES))

        def apply(r, _):
            at = columns(r * LANES, LANES)
            normed[:, at] = (src_ref[:, at].astype(F32) * scale * gain[pl.ds(r, 1), :]).astype(BF16)
            return 0

        lax.fori_loop(0, d // LANES, apply, 0, unroll=4)

    x_copy.wait()
    norm(xbuf, ga_ref)

    def queries(i, _):
        s = arrived(i)
        t = product(normed, s, d).astype(BF16).astype(F32)
        cos, sin = rot_ref[0:1, :], rot_ref[1:2, :]
        for j in range(WIDTH // HEAD):
            one = t[:, j * HEAD : (j + 1) * HEAD]
            turned = one * cos + pltpu.roll(one, HEAD // 2, 1) * sin
            q[pl.ds(i * (WIDTH // HEAD) + j, rows, stride=heads), :] = turned.astype(BF16).astype(F32)
        issue(i + SLOTS, ("kv",))
        return 0

    lax.fori_loop(0, n_q, queries, 0)

    def attend(g, _):
        i = kv0 + 2 * g
        sk = arrived(i)
        sv = arrived(i + 1)
        weights = []
        for t in range(group):
            qb = q[pl.ds(pl.multiple_of((g * group + t) * heads, heads), heads), :]
            zero = jnp.zeros_like(qb)
            both = jnp.concatenate([jnp.concatenate([qb, zero], 1), jnp.concatenate([zero, qb], 1)], 0).astype(BF16)
            keys = ring[sk, t * half_cache : (t + 1) * half_cache]
            scores = lax.dot_general(both, keys, (((1,), (1,)), ((), ())), preferred_element_type=F32) * HEAD**-0.5
            top = jnp.max(scores, -1, keepdims=True)
            top = jnp.maximum(top[:heads], top[heads:])
            e = jnp.exp(scores - jnp.concatenate([top, top], 0))
            total = jnp.sum(e, -1, keepdims=True)
            total = 1.0 / (total[:heads] + total[heads:])
            weights.append((e * jnp.concatenate([total, total], 0)).astype(BF16))
        for t in range(group):
            values = ring[sv, t * half_cache : (t + 1) * half_cache]
            out = jnp.dot(weights[t], values, preferred_element_type=F32)
            seen[pl.ds(g * group + t, heads, stride=rows), :] = out[:heads, :HEAD] + out[heads:, HEAD:]
        issue(i + SLOTS, ("kv", "wo", "gu"))
        issue(i + 1 + SLOTS, ("kv", "wo", "gu"))
        return 0

    lax.fori_loop(0, rows // group, attend, 0)
    for h in range(heads):
        seen_bf[:, h * HEAD : (h + 1) * HEAD] = seen[h * rows : (h + 1) * rows, :].astype(BF16)

    def half_to_partner(ph, c):
        return pltpu.make_async_remote_copy(
            src_ref=sbuf.at[c], dst_ref=dbuf.at[c], send_sem=s_a.at[ph, c], recv_sem=r_a.at[ph, c],
            device_id={"tp": partner}, device_id_type=MESH)

    def term_to(ph, c, dist):
        return pltpu.make_async_remote_copy(
            src_ref=tbuf.at[c, lax.rem(chip + dist, chips)], dst_ref=rbuf.at[c, dist - 1],
            send_sem=s_b.at[ph, c, dist - 1], recv_sem=r_b.at[ph, c, dist - 1],
            device_id={"tp": peer(dist)}, device_id_type=MESH)

    def own_columns(c):
        return columns(c * chunk + core * core_cols + chip * LANES, LANES)

    def result_to(dst, ph, c, dist):
        return pltpu.make_async_remote_copy(
            src_ref=dst.at[:, own_columns(c)], dst_ref=dst.at[:, own_columns(c)],
            send_sem=s_c.at[ph, c, dist - 1], recv_sem=r_c.at[ph, c, dist - 1],
            device_id={"tp": peer(dist)}, device_id_type=MESH)

    def results_to_partner(dst, ph, c):
        at = columns(c * chunk + core * core_cols, core_cols)
        return pltpu.make_async_remote_copy(
            src_ref=dst.at[:, at], dst_ref=dst.at[:, at], send_sem=s_d.at[ph, c], recv_sem=r_d.at[ph, c],
            device_id={"tp": partner}, device_id_type=MESH)

    def stage_a(ph, c):
        sbuf[c] = pbuf[c, 1 - core].astype(BF16)
        half_to_partner(ph, c).start()

    def stage_b(ph, c):
        half_to_partner(ph, c).wait_recv()
        both = pbuf[c, core] + dbuf[c].astype(F32)
        pbuf[c, core] = both
        for p in range(chips):
            tbuf[c, p] = both[:, p * LANES : (p + 1) * LANES].astype(BF16)
        for dist in range(1, chips):
            term_to(ph, c, dist).start()

    def stage_c(ph, c, res, dst):
        for dist in range(1, chips):
            term_to(ph, c, dist).wait_recv()
        total = pbuf[c, core, :, columns(chip * LANES, LANES)]
        for dist in range(1, chips):
            total = total + rbuf[c, dist - 1].astype(F32)
        at = own_columns(c)
        dst[:, at] = (res[:, at].astype(F32) + total).astype(BF16)
        for dist in range(1, chips):
            result_to(dst, ph, c, dist).start()

    def stage_d(ph, c, dst):
        for dist in range(1, chips):
            result_to(dst, ph, c, dist).wait_recv()
        results_to_partner(dst, ph, c).start()

    def finish(ph, c, dst):
        results_to_partner(dst, ph, c).wait()
        half_to_partner(ph, c).wait_send()
        for dist in range(1, chips):
            term_to(ph, c, dist).wait_send()
            result_to(dst, ph, c, dist).wait_send()

    def loop(low, high, body):
        lax.fori_loop(low, high, lambda c, _: (body(c), 0)[1], 0)

    pl.semaphore_wait(barrier, chips)

    def project(w, _):
        i = wo0 + w
        s = arrived(i)
        for m in range(wo_cols // WIDTH):
            c = w * per_item + m * WIDTH // chunk
            at = m * WIDTH % chunk
            part = product(seen_bf, s, qcols, m * qcols)
            pbuf[c, at // core_cols, :, at % core_cols : at % core_cols + WIDTH] = part
            if (m + 1) * WIDTH % chunk == 0:
                stage_a(0, c)
        issue(i + SLOTS, ("gu",))

        @pl.when(w >= 1)
        def _():
            for j in range(per_item):
                stage_b(0, (w - 1) * per_item + j)

        @pl.when(w >= 2)
        def _():
            for j in range(per_item):
                stage_c(0, (w - 2) * per_item + j, xbuf, hbuf)

        return 0

    lax.fori_loop(0, n_wo, project, 0)
    loop((n_wo - 1) * per_item, chunks, lambda c: stage_b(0, c))
    loop((n_wo - 2) * per_item, (n_wo - 1) * per_item, lambda c: stage_c(0, c, xbuf, hbuf))
    loop(0, (n_wo - 2) * per_item, lambda c: stage_d(0, c, hbuf))
    loop((n_wo - 1) * per_item, chunks, lambda c: stage_c(0, c, xbuf, hbuf))
    loop((n_wo - 2) * per_item, chunks, lambda c: stage_d(0, c, hbuf))
    loop(0, chunks, lambda c: finish(0, c, hbuf))
    norm(hbuf, gm_ref)

    def gate_up(j, _):
        i = gu0 + 2 * j
        gate = product(normed, arrived(i), d)
        up = product(normed, arrived(i + 1), d)
        hidden[:, columns(j * WIDTH, WIDTH)] = (gate * (1.0 / (1.0 + jnp.exp(-gate))) * up).astype(BF16)
        issue(i + SLOTS, ("gu", "wd"))
        issue(i + 1 + SLOTS, ("gu", "wd"))
        return 0

    lax.fori_loop(0, ff // WIDTH, gate_up, 0)

    def down(c, _):
        blocks = chunk // WIDTH
        for u in range(blocks):
            i = wd0 + c * blocks + u
            part = product(hidden, arrived(i, ff), ff)
            at = u * WIDTH
            pbuf[c, at // core_cols, :, at % core_cols : at % core_cols + WIDTH] = part
            issue(i + SLOTS, ("wd",))
            if u == blocks // 2 - 1:

                @pl.when(c >= 1)
                def _():
                    stage_b(1, c - 1)

                @pl.when(c >= 2)
                def _():
                    stage_d(1, c - 2, y_ref)

        stage_a(1, c)

        @pl.when(c >= 1)
        def _():
            stage_c(1, c - 1, hbuf, y_ref)

        return 0

    lax.fori_loop(0, chunks, down, 0)
    last = chunks - 1
    stage_b(1, last)
    stage_d(1, last - 1, y_ref)
    stage_c(1, last, hbuf, y_ref)
    stage_d(1, last, y_ref)
    loop(0, chunks, lambda c: finish(1, c, y_ref))


def solution(mesh):
    n = mesh.shape["tp"]

    def step(x, k_cache, v_cache, gain_a, wq, wo, gain_m, w_gate, w_up, w_down):
        (rows, d), cache, qcols, ff = x.shape, k_cache.shape[1], wq.shape[1], w_gate.shape[1]
        half = HEAD // 2
        angle = (cache - 1) * float(THETA) ** (-np.arange(half) / half)
        cos, sin = np.cos(angle), np.sin(angle)
        rot = jnp.asarray(np.stack([np.concatenate([cos, cos]), np.concatenate([-sin, sin])]), F32)
        chips = n // CORES
        chunk = n * LANES
        chunks = d // chunk
        core_cols = chips * LANES
        any_, vmem = pl.BlockSpec(memory_space=pl.ANY), pl.BlockSpec(memory_space=pltpu.VMEM)
        dma = pltpu.SemaphoreType.DMA
        flops = 2 * rows * (2 * d * qcols + 3 * d * ff + 2 * cache * qcols)
        return pl.pallas_call(
            functools.partial(layer, n, (rows, d, cache, qcols, ff)),
            out_shape=jax.ShapeDtypeStruct((rows, d), BF16),
            in_specs=[any_, any_, any_, vmem, vmem, vmem] + [any_] * 5,
            out_specs=vmem,
            scratch_shapes=[
                pltpu.VMEM((SLOTS, d, WIDTH), BF16),
                pltpu.VMEM((rows, d), BF16),
                pltpu.VMEM((rows, d), BF16),
                pltpu.VMEM((rows, d), BF16),
                pltpu.VMEM((d // LANES, LANES), F32),
                pltpu.VMEM((rows * (qcols // HEAD), HEAD), F32),
                pltpu.VMEM((rows * (qcols // HEAD), HEAD), F32),
                pltpu.VMEM((rows, qcols), BF16),
                pltpu.VMEM((rows, ff), BF16),
                pltpu.VMEM((chunks, CORES, rows, core_cols), F32),
                pltpu.VMEM((chunks, rows, core_cols), BF16),
                pltpu.VMEM((chunks, rows, core_cols), BF16),
                pltpu.VMEM((chunks, chips, rows, LANES), BF16),
                pltpu.VMEM((chunks, chips - 1, rows, LANES), BF16),
                dma((SLOTS,)),
                dma(()),
                dma((2, chunks)),
                dma((2, chunks)),
                dma((2, chunks, chips - 1)),
                dma((2, chunks, chips - 1)),
                dma((2, chunks, chips - 1)),
                dma((2, chunks, chips - 1)),
                dma((2, chunks)),
                dma((2, chunks)),
            ],
            compiler_params=pltpu.CompilerParams(
                collective_id=0, has_side_effects=True, vmem_limit_bytes=67_043_328
            ),
            cost_estimate=pl.CostEstimate(
                flops=flops, transcendentals=0, bytes_accessed=2 * (2 * d * qcols + 3 * d * ff + 2 * rows * cache * HEAD)
            ),
        )(
            x,
            k_cache.reshape(rows, cache, HEAD),
            v_cache.reshape(rows, cache, HEAD),
            gain_a.reshape(d // LANES, LANES),
            gain_m.reshape(d // LANES, LANES),
            rot,
            wq,
            wo,
            w_gate,
            w_up,
            w_down,
        )

    states, cache, columns, rows_of = P("dp", None), P("dp", None, "tp", None), P(None, "tp"), P("tp", None)
    return jax.shard_map(
        step,
        mesh=mesh,
        in_specs=(states, cache, cache, P(None), columns, rows_of, P(None), columns, columns, rows_of),
        out_specs=states,
        check_vma=False,
    )
```

time: 310 us -> 196 us (0.63)
  Pallas kernels: 0 us -> 194 us
  matrix products: 178 us -> 0 us
  waiting for transfers between devices: 109 us -> 0 us
  between operations: 13.5 us -> 0.01 us
  other arithmetic: 6.58 us -> 0 us
    pallas_call x0 -> x1, Pallas kernels: none -> 194 us  [step(): pl.pallas_call(functools.partial(layer, n, (rows, d, cache, qcols, ff)),...]
    dot_general x6 -> x0, matrix products: 149 us -> none  [the longest x1 35.5 us: step(): jnp.dot(hidden_of(normed(h, gain_m), w_gate, w_up), w_down, preferred_ele...]
    psum x2 -> x0, waiting for transfers between devices: 109 us -> none  [added(): lax.psum(term.astype(jnp.bfloat16), 'tp').astype(jnp.float32)]
    sub x1 -> x0, matrix products: 29.1 us -> none  [seen_by(): weights = jax.nn.softmax(scores, -1).astype(jnp.bfloat16)]
    reduce_sum x2 -> x0, other arithmetic: 3.22 us -> none  [normed(): scale = lax.rsqrt(jnp.mean(wide * wide, -1, keepdims=True) + 1e-06)]
    convert_element_type x3 -> x0, other arithmetic: 3.16 us -> none  [the longest x1 2.43 us: added(): (t.astype(jnp.float32) + lax.psum(term.astype(jnp.bfloat16), 'tp').astype...]
  transfers between devices with their start and end apart: 2 -> 0, of which waited for: 2 -> 0; matrix products, arithmetic and copies ran while one was open for 0% -> 0% of each run, Pallas kernels for 0% -> 0%
where the time goes in v1:
time: 196 us
  Pallas kernels  194 us (99%)
  local copies, waits for them, and re-layouts  2.26 us (1%)
    pallas_call x1, Pallas kernels, step(): pl.pallas_call(functools.partial(layer, n, (rows, d, cache, qcols, ff)),...  194 us

profile of v1, /device:TPU:113, one launch (start us, length us, event | category | flops | bytes accessed | tf_op | source)
XLA Modules:
  0.0 195.8 jit_solution(8752791288414467295)
XLA Ops:
  0.0 193.5 %shard_map.109 = bf16[64,8192]{1,0:T(8,128)(2,1)} custom-call(bf16[64,8192]{1,0:T(8,128)(2,1)} %x_hbm.1, bf16[64,4096,128]{2,1,0:T(8,128)(2,1)} %bitcast.k_hbm, bf16[64,4096,128]{2,1,0:T(8,128)(2,1)} %bitcast.1.v_hbm, bf16[64,128]{1,0:T(8,128)(2,1)} %bitcast.4, bf16[64,128]{1,0:T(8,128)(2,1)} %bitcast.5, f32[2,128]{1,0:T(2,128)} %constant.2.clone.rot_ref, ...), custom_call_target="tpu_custom_call" | custom-call | flops 22548578304 | bytes 469762048 | tf_op jit(solution)/shard_map/pallas_call | solution.py:351
  193.5 2.3 %copy.13 = bf16[64,8192]{1,0:T(8,128)(2,1)} copy(bf16[64,8192]{1,0:T(8,128)(2,1)} %shard_map.109) | data formatting | bytes 2097152

commit v2 on v1

--- a/solution.py
+++ b/solution.py
@@ -13,6 +13,7 @@
 LANES = 128
 WIDTH = 256
 SLOTS = 12
+STEP = 256
 CORES = 2
 F32, BF16 = jnp.float32, jnp.bfloat16
 MESH = pl.DeviceIdType.MESH
@@ -105,13 +106,15 @@
         pltpu.make_async_copy(src.at[:, pl.ds(0, WIDTH)], ring.at[s, pl.ds(0, height)], ring_sem.at[s]).wait()
         return s
 
-    def product(a_ref, s, depth, start=0, step=2048):
-        total = None
+    def products(a_ref, depth, first, second, step=STEP):
+        totals = [None, None]
         for k in range(0, depth, step):
             size = min(step, depth - k)
-            part = jnp.dot(a_ref[:, k : k + size], ring[s, start + k : start + k + size], preferred_element_type=F32)
-            total = part if total is None else total + part
-        return total
+            a = a_ref[:, k : k + size]
+            for j, (s, start) in enumerate((first, second)):
+                part = jnp.dot(a, ring[s, start + k : start + k + size], preferred_element_type=F32)
+                totals[j] = part if totals[j] is None else totals[j] + part
+        return totals
 
     barrier = pltpu.get_barrier_semaphore()
     for device in [partner] + [peer(dist) for dist in range(1, chips)]:
@@ -144,18 +147,20 @@
     x_copy.wait()
     norm(xbuf, ga_ref)
 
-    def queries(i, _):
-        s = arrived(i)
-        t = product(normed, s, d).astype(BF16).astype(F32)
+    def queries(p, _):
+        i = 2 * p
+        both = products(normed, d, (arrived(i), 0), (arrived(i + 1), 0))
         cos, sin = rot_ref[0:1, :], rot_ref[1:2, :]
-        for j in range(WIDTH // HEAD):
-            one = t[:, j * HEAD : (j + 1) * HEAD]
-            turned = one * cos + pltpu.roll(one, HEAD // 2, 1) * sin
-            q[pl.ds(i * (WIDTH // HEAD) + j, rows, stride=heads), :] = turned.astype(BF16).astype(F32)
-        issue(i + SLOTS, ("kv",))
+        for b, t in enumerate(both):
+            t = t.astype(BF16).astype(F32)
+            for j in range(WIDTH // HEAD):
+                one = t[:, j * HEAD : (j + 1) * HEAD]
+                turned = one * cos + pltpu.roll(one, HEAD // 2, 1) * sin
+                q[pl.ds((i + b) * (WIDTH // HEAD) + j, rows, stride=heads), :] = turned.astype(BF16).astype(F32)
+            issue(i + b + SLOTS, ("kv",))
         return 0
 
-    lax.fori_loop(0, n_q, queries, 0)
+    lax.fori_loop(0, n_q // 2, queries, 0)
 
     def attend(g, _):
         i = kv0 + 2 * g
@@ -256,12 +261,12 @@
     def project(w, _):
         i = wo0 + w
         s = arrived(i)
-        for m in range(wo_cols // WIDTH):
+        for m in range(0, wo_cols // WIDTH, 2):
             c = w * per_item + m * WIDTH // chunk
-            at = m * WIDTH % chunk
-            part = product(seen_bf, s, qcols, m * qcols)
-            pbuf[c, at // core_cols, :, at % core_cols : at % core_cols + WIDTH] = part
-            if (m + 1) * WIDTH % chunk == 0:
+            for b, part in enumerate(products(seen_bf, qcols, (s, m * qcols), (s, (m + 1) * qcols))):
+                at = (m + b) * WIDTH % chunk
+                pbuf[c, at // core_cols, :, at % core_cols : at % core_cols + WIDTH] = part
+            if (m + 2) * WIDTH % chunk == 0:
                 stage_a(0, c)
         issue(i + SLOTS, ("gu",))
 
@@ -288,8 +293,7 @@
 
     def gate_up(j, _):
         i = gu0 + 2 * j
-        gate = product(normed, arrived(i), d)
-        up = product(normed, arrived(i + 1), d)
+        gate, up = products(normed, d, (arrived(i), 0), (arrived(i + 1), 0))
         hidden[:, columns(j * WIDTH, WIDTH)] = (gate * (1.0 / (1.0 + jnp.exp(-gate))) * up).astype(BF16)
         issue(i + SLOTS, ("gu", "wd"))
         issue(i + 1 + SLOTS, ("gu", "wd"))
@@ -299,13 +303,14 @@
 
     def down(c, _):
         blocks = chunk // WIDTH
-        for u in range(blocks):
+        for u in range(0, blocks, 2):
             i = wd0 + c * blocks + u
-            part = product(hidden, arrived(i, ff), ff)
-            at = u * WIDTH
-            pbuf[c, at // core_cols, :, at % core_cols : at % core_cols + WIDTH] = part
+            for b, part in enumerate(products(hidden, ff, (arrived(i, ff), 0), (arrived(i + 1, ff), 0))):
+                at = (u + b) * WIDTH
+                pbuf[c, at // core_cols, :, at % core_cols : at % core_cols + WIDTH] = part
             issue(i + SLOTS, ("wd",))
-            if u == blocks // 2 - 1:
+            issue(i + 1 + SLOTS, ("wd",))
+            if u == 0:
 
                 @pl.when(c >= 1)
                 def _():
@@ -313,19 +318,20 @@
 
                 @pl.when(c >= 2)
                 def _():
-                    stage_d(1, c - 2, y_ref)
+                    stage_c(1, c - 2, hbuf, y_ref)
+
+                @pl.when(c >= 3)
+                def _():
+                    stage_d(1, c - 3, y_ref)
 
         stage_a(1, c)
-
-        @pl.when(c >= 1)
-        def _():
-            stage_c(1, c - 1, hbuf, y_ref)
-
         return 0
 
     lax.fori_loop(0, chunks, down, 0)
     last = chunks - 1
+    stage_c(1, last - 1, hbuf, y_ref)
     stage_b(1, last)
+    stage_d(1, last - 2, y_ref)
     stage_d(1, last - 1, y_ref)
     stage_c(1, last, hbuf, y_ref)
     stage_d(1, last, y_ref)

time: 196 us -> 167 us (0.85)
  Pallas kernels: 194 us -> 164 us
    pallas_call x1, Pallas kernels: 194 us -> 164 us  [step(): pl.pallas_call(functools.partial(layer, n, (rows, d, cache, qcols, ff)),...]
where the time goes in v2:
time: 167 us; the launch traced here: 166 us
  Pallas kernels  164 us (98%)
  local copies, waits for them, and re-layouts  2.26 us (1%)
    pallas_call x1, Pallas kernels, step(): pl.pallas_call(functools.partial(layer, n, (rows, d, cache, qcols, ff)),...  164 us

profile of v2, /device:TPU:113, one launch (start us, length us, event | category | flops | bytes accessed | tf_op | source)
XLA Modules:
  0.0 166.5 jit_solution(9900381232828315406)
XLA Ops:
  0.0 164.2 %shard_map.109 = bf16[64,8192]{1,0:T(8,128)(2,1)} custom-call(bf16[64,8192]{1,0:T(8,128)(2,1)} %x_hbm.1, bf16[64,4096,128]{2,1,0:T(8,128)(2,1)} %bitcast.k_hbm, bf16[64,4096,128]{2,1,0:T(8,128)(2,1)} %bitcast.1.v_hbm, bf16[64,128]{1,0:T(8,128)(2,1)} %bitcast.4, bf16[64,128]{1,0:T(8,128)(2,1)} %bitcast.5, f32[2,128]{1,0:T(2,128)} %constant.2.clone.rot_ref, ...), custom_call_target="tpu_custom_call" | custom-call | flops 22548578304 | bytes 469762048 | tf_op jit(solution)/shard_map/pallas_call | solution.py:357
  164.2 2.3 %copy.13 = bf16[64,8192]{1,0:T(8,128)(2,1)} copy(bf16[64,8192]{1,0:T(8,128)(2,1)} %shard_map.109) | data formatting | bytes 2097152

commit v3 on v2

--- a/solution.py
+++ b/solution.py
@@ -275,19 +275,15 @@
             for j in range(per_item):
                 stage_b(0, (w - 1) * per_item + j)
 
-        @pl.when(w >= 2)
-        def _():
-            for j in range(per_item):
-                stage_c(0, (w - 2) * per_item + j, xbuf, hbuf)
-
         return 0
 
     lax.fori_loop(0, n_wo, project, 0)
     loop((n_wo - 1) * per_item, chunks, lambda c: stage_b(0, c))
-    loop((n_wo - 2) * per_item, (n_wo - 1) * per_item, lambda c: stage_c(0, c, xbuf, hbuf))
-    loop(0, (n_wo - 2) * per_item, lambda c: stage_d(0, c, hbuf))
-    loop((n_wo - 1) * per_item, chunks, lambda c: stage_c(0, c, xbuf, hbuf))
-    loop((n_wo - 2) * per_item, chunks, lambda c: stage_d(0, c, hbuf))
+    late = (n_wo - 1) * per_item
+    loop(0, late, lambda c: stage_c(0, c, xbuf, hbuf))
+    loop(0, late - per_item, lambda c: stage_d(0, c, hbuf))
+    loop(late, chunks, lambda c: stage_c(0, c, xbuf, hbuf))
+    loop(late - per_item, chunks, lambda c: stage_d(0, c, hbuf))
     loop(0, chunks, lambda c: finish(0, c, hbuf))
     norm(hbuf, gm_ref)
 
@@ -310,30 +306,30 @@
                 pbuf[c, at // core_cols, :, at % core_cols : at % core_cols + WIDTH] = part
             issue(i + SLOTS, ("wd",))
             issue(i + 1 + SLOTS, ("wd",))
-            if u == 0:
-
-                @pl.when(c >= 1)
-                def _():
-                    stage_b(1, c - 1)
-
-                @pl.when(c >= 2)
-                def _():
-                    stage_c(1, c - 2, hbuf, y_ref)
-
-                @pl.when(c >= 3)
-                def _():
-                    stage_d(1, c - 3, y_ref)
 
         stage_a(1, c)
+
+        @pl.when(c >= 1)
+        def _():
+            stage_b(1, c - 1)
+
+        @pl.when(c >= 2)
+        def _():
+            stage_c(1, c - 2, hbuf, y_ref)
+
+        @pl.when(c >= 3)
+        def _():
+            stage_d(1, c - 3, y_ref)
+
         return 0
 
     lax.fori_loop(0, chunks, down, 0)
     last = chunks - 1
+    stage_b(1, last)
     stage_c(1, last - 1, hbuf, y_ref)
-    stage_b(1, last)
     stage_d(1, last - 2, y_ref)
+    stage_c(1, last, hbuf, y_ref)
     stage_d(1, last - 1, y_ref)
-    stage_c(1, last, hbuf, y_ref)
     stage_d(1, last, y_ref)
     loop(0, chunks, lambda c: finish(1, c, y_ref))
 

time: 167 us -> 165 us (0.988)
  Pallas kernels: 164 us -> 162 us
    pallas_call x1, Pallas kernels: 164 us -> 162 us  [step(): pl.pallas_call(functools.partial(layer, n, (rows, d, cache, qcols, ff)),...]
where the time goes in v3:
time: 165 us; the launch traced here: 164 us
  Pallas kernels  162 us (98%)
  local copies, waits for them, and re-layouts  2.26 us (1%)
    pallas_call x1, Pallas kernels, step(): pl.pallas_call(functools.partial(layer, n, (rows, d, cache, qcols, ff)),...  162 us

profile of v3, /device:TPU:113, one launch (start us, length us, event | category | flops | bytes accessed | tf_op | source)
XLA Modules:
  0.0 164.4 jit_solution(16079672657899413320)
XLA Ops:
  0.0 162.2 %shard_map.109 = bf16[64,8192]{1,0:T(8,128)(2,1)} custom-call(bf16[64,8192]{1,0:T(8,128)(2,1)} %x_hbm.1, bf16[64,4096,128]{2,1,0:T(8,128)(2,1)} %bitcast.k_hbm, bf16[64,4096,128]{2,1,0:T(8,128)(2,1)} %bitcast.1.v_hbm, bf16[64,128]{1,0:T(8,128)(2,1)} %bitcast.4, bf16[64,128]{1,0:T(8,128)(2,1)} %bitcast.5, f32[2,128]{1,0:T(2,128)} %constant.2.clone.rot_ref, ...), custom_call_target="tpu_custom_call" | custom-call | flops 22548578304 | bytes 469762048 | tf_op jit(solution)/shard_map/pallas_call | solution.py:353
  162.2 2.3 %copy.13 = bf16[64,8192]{1,0:T(8,128)(2,1)} copy(bf16[64,8192]{1,0:T(8,128)(2,1)} %shard_map.109) | data formatting | bytes 2097152
